TPU v7x, 256 devices: a whole 4x4x8 slice. The times are simulated.
256 devices in a mesh: rep: 4 (over y), row: 16 (over z, core), col: 4 (over x).
Axes of the slice: x: 4, y: 4, z: 8, core: 2. Of those that a mesh axis runs over, the one named last changes fastest.
Arguments:
- acts: bfloat16 [4, 256, 5120], P('rep', None, 'row'), may hold values from -6 to 6
- grad_out: bfloat16 [4, 256, 13824], P('rep', None, 'col'), may hold values from -0.375 to 0.375
- momentum: bfloat16 [4, 5120, 13824], P('rep', 'row', 'col'), may hold values from -6 to 6
- q_basis: bfloat16 [640, 13824], P(None, 'col'), may hold values from -6 to 6
Outputs:
- momentum_next: bfloat16 [4, 5120, 13824], P('rep', 'row', 'col')
- q_next: bfloat16 [640, 13824], P('row', 'col')
- update: bfloat16 [5120, 13824], P('row', 'col')
All inputs are finite; a program needn't handle non-finite values.
Results may differ from a plain program's by a relative error of at most 0.019.
Values may be sent and summed in bfloat16 or wider, within the bound.
No kernel may reach another device: no remote copies, remote signals or barrier semaphores. Data moves between devices by JAX's collectives and lax.ppermute only.
A program may use at most 128 MiB of HBM per device.

v0:
```python
import jax
import jax.numpy as jnp
from jax import lax
from jax.sharding import Mesh
from jax.sharding import PartitionSpec as P

RANK = 640
ROW = ("row_0", "row_1")


keep_factor = 0.6


def in_blocks(x, dim, peers):
    lengths = x.shape
    parts = x.reshape(*lengths[:dim], peers, lengths[dim] // peers, *lengths[dim + 1 :])
    return jnp.moveaxis(parts, dim, 0)


def sum_at_owner(x, axis, dim):
    peers = lax.axis_size(axis)
    parts = lax.all_to_all(in_blocks(x, dim, peers), axis, 0, 0, tiled=True)
    return jnp.sum(parts, axis=0)


def padded_to(lines, peers):
    spare = -lines.shape[0] % peers
    if not spare:
        return lines
    return jnp.concatenate([lines, jnp.zeros((spare, *lines.shape[1:]), lines.dtype)])


def sent_to_all(x, axis):
    peers = lax.axis_size(axis)
    return lax.all_to_all(jnp.broadcast_to(x[None], (peers, *x.shape)), axis, 0, 0, tiled=True)


def laid_out(parts, dim):
    parts = jnp.moveaxis(parts, 0, dim)
    lengths = parts.shape
    return parts.reshape(*lengths[:dim], lengths[dim] * lengths[dim + 1], *lengths[dim + 2 :])


def gathered_by_axis(x, axes, dim):
    far, near = axes
    parts = sent_to_all(sent_to_all(x, far), near)
    return laid_out(parts.swapaxes(0, 1).reshape(-1, *x.shape), dim)


def sum_in_two_steps(x, axes, dim):
    far, near = axes
    own = sum_at_owner(in_blocks(x, dim, lax.axis_size(far)), near, dim + 1)
    return jnp.sum(lax.all_to_all(own, far, 0, 0, tiled=True), axis=0)


def sum_by_parts(x, axes):
    lines = x.reshape(-1)
    padded = padded_to(lines, lax.axis_size(axes[0]) * lax.axis_size(axes[1]))
    whole = gathered_by_axis(sum_in_two_steps(padded, axes, 0), axes, 0)
    return lax.slice_in_dim(whole, 0, len(lines)).reshape(x.shape)


def gather_directly(x, axis, dim):
    return laid_out(sent_to_all(x, axis), dim)


def sum_at_owner_2(x, axis, dim):
    peers = lax.axis_size(axis)
    parts = lax.all_to_all(in_blocks(x, dim, peers), axis, 0, 0, tiled=True)
    return jnp.sum(parts.astype(jnp.float32), axis=0)


def sum_in_two_steps_2(x, axes, dim):
    far, near = axes
    parts = in_blocks(x, dim, lax.axis_size(far))
    nearer = sum_at_owner_2(parts, near, dim + 1)
    arrived = lax.all_to_all(
        nearer.astype(jnp.bfloat16), far, split_axis=0, concat_axis=0, tiled=True
    )
    return arrived.astype(jnp.float32).sum(axis=0)


def over_copies(x, axis):
    return sent_to_all(x, axis).astype(jnp.float32).sum(axis=0)


def of_everyone(x, axis):
    everything = sent_to_all(x, axis)
    return jnp.sum(everything, axis=0)


def orthonormal(left, gram):
    chol = jnp.linalg.cholesky(gram)
    return lax.linalg.triangular_solve(
        chol, left, left_side=False, lower=True, transpose_a=True
    ).astype(jnp.bfloat16)


def shards(acts, grad_out, momentum, q_basis):
    grad = lax.dot_general(
        acts[0], grad_out[0], (((0,), (0,)), ((), ())), preferred_element_type=jnp.float32
    )
    boosted = (momentum[0].astype(jnp.float32) + grad).astype(jnp.bfloat16)
    partial_value = lax.dot_general(
        boosted, q_basis, (((1,), (1,)), ((), ())), preferred_element_type=jnp.float32
    )
    share = sum_at_owner(partial_value, ("rep", "col"), 0)
    gram = sum_by_parts(
        jnp.dot(share.T, share, precision=lax.Precision.HIGHEST),
        (("rep", "row_0"), ("row_1", "col")),
    )
    ortho = gather_directly(orthonormal(share, gram), ("rep", "col"), 0)
    replicas = lax.axis_size("rep")
    summed = sum_in_two_steps_2(
        lax.dot_general(
            ortho, boosted, (((0,), (0,)), ((), ())), preferred_element_type=jnp.float32
        ).astype(jnp.bfloat16),
        ("row_0", "row_1"),
        0,
    )
    summed = over_copies(summed.astype(jnp.bfloat16), "rep").astype(jnp.float32)
    piece = (summed * (1.0 / replicas)).astype(jnp.bfloat16)
    right = gathered_by_axis(piece, ("row_0", "row_1"), 0)
    right_wide = right.astype(jnp.float32)
    columns_all = right.shape[1] * lax.axis_size("col")
    squares = of_everyone(jnp.sum(right_wide * right_wide, axis=1), "col")
    msq = squares / columns_all
    q_full = (right_wide * lax.rsqrt(msq + 1e-06)[:, None]).astype(jnp.bfloat16)
    block = RANK // lax.axis_size(ROW)
    q_next = lax.dynamic_slice_in_dim(q_full, lax.axis_index(ROW) * block, block, 0)
    feedback = jnp.dot(ortho, right, preferred_element_type=jnp.float32)
    momentum_next = (boosted.astype(jnp.float32) - (1.0 - keep_factor) * feedback).astype(
        jnp.bfloat16
    )[None]
    width_all = boosted.shape[0] * lax.axis_size(ROW)
    update = (
        jnp.sqrt(jnp.float32(width_all) / RANK)
        * jnp.dot(ortho, q_full, preferred_element_type=jnp.float32)
    ).astype(jnp.bfloat16)
    return (momentum_next, q_next, update)


def solution(mesh):
    split = Mesh(
        mesh.devices.reshape(mesh.shape["rep"], 8, 2, mesh.shape["col"]),
        ("rep", "row_0", "row_1", "col"),
    )
    return jax.shard_map(
        shards,
        mesh=split,
        in_specs=(P("rep", None, ROW), P("rep", None, "col"), P("rep", ROW, "col"), P(None, "col")),
        out_specs=(P("rep", ROW, "col"), P(ROW, "col"), P(ROW, "col")),
        check_vma=False,
    )
```

profile of v0, /device:TPU:1, one launch (start us, length us, event | category | flops | bytes accessed | tf_op | source)
XLA Modules:
  0.0 512.9 jit_solution(5209678288642751774)
XLA Ops:
  0.6 1.5 copy-done
  2.1 2.6 fusion.5
  4.7 1.3 copy-done.3
  6.1 2.0 fusion.54
  8.2 23.0 %all_to_all.66 = f32[16,20,640]{2,1,0:T(8,128)S(1)} all-to-all(f32[16,20,640]{2,1,0:T(8,128)S(1)} %reshape.137), channel_id=1, replica_groups=mesh['rep'=4,'row_0'=8,'row_1'=2,'col'=4] {'rep','col'}, dimensions={0} | all-to-all | bytes 1638400 | tf_op jit(solution)/shard_map/all_to_all | solution.py:22
  31.2 1.5 fusion.55
  34.2 26.2 %all_to_all.67 = f32[8,32,1600]{2,1,0:T(8,128)S(1)} all-to-all(f32[8,32,1600]{2,1,0:T(8,128)S(1)} %bitcast.105), channel_id=1, replica_groups=mesh['rep'=4,'row_0'=8,'row_1'=2,'col'=4] {'row_1','col'}, dimensions={0} | all-to-all | bytes 3276800 | tf_op jit(solution)/shard_map/all_to_all | solution.py:22
  60.7 18.2 %all_to_all.68 = f32[32,1,1600]{2,1,0:T(1,128)S(1)} all-to-all(f32[32,1,1600]{2,1,0:T(1,128)S(1)} %all_to_all.43), channel_id=1, replica_groups=mesh['rep'=4,'row_0'=8,'row_1'=2,'col'=4] {'rep','row_0'}, dimensions={0} | all-to-all | bytes 409600 | tf_op jit(solution)/shard_map/all_to_all | solution.py:53
  79.2 15.0 %all_to_all.69 = f32[32,1,1600]{2,1,0:T(1,128)S(1)} all-to-all(f32[32,1,1600]{2,1,0:T(1,128)S(1)} %broadcast_in_dim.22), channel_id=1, replica_groups=mesh['rep'=4,'row_0'=8,'row_1'=2,'col'=4] {'rep','row_0'}, dimensions={0} | all-to-all | bytes 409600 | tf_op jit(solution)/shard_map/all_to_all | solution.py:35
  95.5 6.6 %all-to-all-start.4 = ((f32[8,32,1600]{2,1,0:T(8,128)}), f32[8,32,1600]{2,1,0:T(8,128)S(1)}, u32[]{:S(2)}, u32[]{:S(2)}) async-start(f32[8,32,1600]{2,1,0:T(8,128)} %broadcast_in_dim.24), calls=%async_computation.4 | async-start | bytes 3407872 | tf_op jit(solution)/shard_map/all_to_all | solution.py:35
  102.1 22.0 %all-to-all-done.4 = f32[8,32,1600]{2,1,0:T(8,128)S(1)} async-done(((f32[8,32,1600]{2,1,0:T(8,128)}), f32[8,32,1600]{2,1,0:T(8,128)S(1)}, u32[]{:S(2)}, u32[]{:S(2)}) %all-to-all-start.4) | async-done | bytes 1638432 | tf_op jit(solution)/shard_map/all_to_all | solution.py:35
  126.2 1.6 copy.25
  129.1 11.7 %cholesky.133 = f32[128,128]{1,0:T(8,128)S(1)} custom-call(f32[128,128]{1,0:T(8,128)S(1)} %cholesky.340), custom_call_target="Cholesky" | custom-call | tf_op jit(solution)/shard_map/jit(cholesky)/cholesky | solution.py:93
  141.0 9.8 %custom-call.38 = f32[1,128,128]{1,2,0:T(8,128)S(1)} custom-call(f32[1,128,128]{2,1,0:T(8,128)S(1)} %get-tuple-element.33), custom_call_target="InvertDiagBlocksLowerTriangular" | custom-call | tf_op jit(solution)/shard_map/jit(cholesky)/cholesky | solution.py:93
  152.3 11.7 %cholesky.272 = f32[128,128]{1,0:T(8,128)S(1)} custom-call(f32[128,128]{1,0:T(8,128)S(1)} %cholesky.344), custom_call_target="Cholesky" | custom-call | tf_op jit(solution)/shard_map/jit(cholesky)/cholesky | solution.py:93
  164.0 10.0 %custom-call.39 = f32[1,128,128]{1,2,0:T(8,128)S(1)} custom-call(f32[1,128,128]{2,1,0:T(8,128)S(1)} %get-tuple-element.30), custom_call_target="InvertDiagBlocksLowerTriangular" | custom-call | tf_op jit(solution)/shard_map/jit(cholesky)/cholesky | solution.py:93
  176.4 11.7 %cholesky.293 = f32[128,128]{1,0:T(8,128)S(1)} custom-call(f32[128,128]{1,0:T(8,128)S(1)} %cholesky.349), custom_call_target="Cholesky" | custom-call | tf_op jit(solution)/shard_map/jit(cholesky)/cholesky | solution.py:93
  188.2 9.8 %custom-call.40 = f32[1,128,128]{1,2,0:T(8,128)S(1)} custom-call(f32[1,128,128]{2,1,0:T(8,128)S(1)} %get-tuple-element.27), custom_call_target="InvertDiagBlocksLowerTriangular" | custom-call | tf_op jit(solution)/shard_map/jit(cholesky)/cholesky | solution.py:93
  200.3 12.5 %cholesky.312 = f32[128,128]{1,0:T(8,128)S(1)} custom-call(f32[128,128]{1,0:T(8,128)} %cholesky.354), custom_call_target="Cholesky" | custom-call | tf_op jit(solution)/shard_map/jit(cholesky)/cholesky | solution.py:93
  213.7 10.6 %custom-call.41 = f32[1,128,128]{1,2,0:T(8,128)S(1)} custom-call(f32[1,128,128]{2,1,0:T(8,128)} %get-tuple-element.24), custom_call_target="InvertDiagBlocksLowerTriangular" | custom-call | tf_op jit(solution)/shard_map/jit(cholesky)/cholesky | solution.py:93
  224.9 11.7 %cholesky.329 = f32[128,128]{1,0:T(8,128)S(1)} custom-call(f32[128,128]{1,0:T(8,128)S(1)} %convolution_subtract_fusion.3), custom_call_target="Cholesky" | custom-call | tf_op jit(solution)/shard_map/jit(cholesky)/cholesky | solution.py:93
  242.5 13.0 %while.1 = (s32[]{:T(128)}, f32[640,640]{1,0:T(8,128)S(1)}, s32[5,2]{0,1:T(2,128)S(1)}, f32[5,128,128]{2,1,0:T(8,128)}, s32[]{:T(128)}) while((s32[]{:T(128)}, f32[640,640]{1,0:T(8,128)S(1)}, s32[5,2]{0,1:T(2,128)S(1)}, f32[5,128,128]{2,1,0:T(8,128)}, s32[]{:T(128)}) %tuple.37), condition=%wide.while_cond, body=%wide.while_body.sunk | while | flops 2 | bytes 132205 | solution.py:94
  243.1 2.0 bitcast_dynamic-update-slice_fusion.2
  245.7 2.0 bitcast_dynamic-update-slice_fusion.2
  248.3 2.0 bitcast_dynamic-update-slice_fusion.2
  250.9 2.0 bitcast_dynamic-update-slice_fusion.2
  253.5 2.0 bitcast_dynamic-update-slice_fusion.2
  255.5 49.9 %custom-call.42 = f32[5,128,128]{1,2,0:T(8,128)S(1)} custom-call(f32[5,128,128]{2,1,0:T(8,128)} %get-tuple-element.10), custom_call_target="InvertDiagBlocksLowerTriangular" | custom-call | tf_op jit(solution)/shard_map/triangular_solve | solution.py:94
  307.6 13.5 %all_to_all.70 = bf16[16,20,640]{2,1,0:T(8,128)(2,1)S(1)} all-to-all(bf16[16,20,640]{2,1,0:T(8,128)(2,1)S(1)} %broadcast_in_dim.25), channel_id=1, replica_groups=mesh['rep'=4,'row_0'=8,'row_1'=2,'col'=4] {'rep','col'}, dimensions={0} | all-to-all | bytes 819200 | tf_op jit(solution)/shard_map/all_to_all | solution.py:35
  321.1 4.2 convolution_convert_fusion
  325.6 10.0 %all_to_all.71 = bf16[2,8,40,3456]{3,2,1,0:T(8,128)(2,1)} all-to-all(bf16[2,8,40,3456]{3,2,1,0:T(8,128)(2,1)S(1)} %bitcast.103), channel_id=1, replica_groups=mesh['rep'=4,'row_0'=8,'row_1'=2,'col'=4] {'row_1'}, dimensions={0} | all-to-all | bytes 8847360 | tf_op jit(solution)/shard_map/all_to_all | solution.py:69
  335.7 5.0 reduce_sum.81
  340.6 58.4 %all_to_all.72 = bf16[8,40,3456]{2,1,0:T(8,128)(2,1)} all-to-all(bf16[8,40,3456]{2,1,0:T(8,128)(2,1)} %reduce_sum.81), channel_id=1, replica_groups=mesh['rep'=4,'row_0'=8,'row_1'=2,'col'=4] {'row_0'}, dimensions={0} | all-to-all | bytes 4423680 | tf_op jit(solution)/shard_map/all_to_all | solution.py:77
  399.1 2.0 reduce_sum.82
  401.1 17.6 %all_to_all.73 = bf16[4,40,3456]{2,1,0:T(8,128)(2,1)S(1)} all-to-all(bf16[4,40,3456]{2,1,0:T(8,128)(2,1)S(1)} %broadcast_in_dim.26), channel_id=1, replica_groups=mesh['rep'=4,'row_0'=8,'row_1'=2,'col'=4] {'rep'}, dimensions={0} | all-to-all | bytes 2211840 | tf_op jit(solution)/shard_map/all_to_all | solution.py:35
  418.9 1.5 broadcast_in_dim.27
  420.4 4.4 all-to-all-start.9
  424.8 50.8 %all-to-all-done.9 = bf16[8,40,3456]{2,1,0:T(8,128)(2,1)} async-done(((bf16[8,40,3456]{2,1,0:T(8,128)(2,1)}), bf16[8,40,3456]{2,1,0:T(8,128)(2,1)}, u32[]{:S(2)}, u32[]{:S(2)}) %all-to-all-start.9) | async-done | bytes 2211872 | tf_op jit(solution)/shard_map/all_to_all | solution.py:35
  475.6 1.9 broadcast_in_dim.28
  477.5 10.8 %all_to_all.74 = bf16[2,8,40,3456]{3,2,1,0:T(8,128)(2,1)S(1)} all-to-all(bf16[2,8,40,3456]{3,2,1,0:T(8,128)(2,1)S(1)} %broadcast_in_dim.28), channel_id=1, replica_groups=mesh['rep'=4,'row_0'=8,'row_1'=2,'col'=4] {'row_1'}, dimensions={0} | all-to-all | bytes 8847360 | tf_op jit(solution)/shard_map/all_to_all | solution.py:35
  488.3 2.0 copy-done.2
  491.9 3.5 all-to-all-start.11
  495.5 2.7 copy.27
  498.2 2.1 copy-done.5
  500.3 3.3 fusion.6
  503.9 1.8 multiply_convert_fusion
  505.6 3.5 fusion.1
  509.1 3.3 fusion.4
  (90 shorter events, 24.7 us)
Async XLA Ops:
  0.6 1.5 copy-start
  2.1 4.0 copy-start.10
  4.7 1.4 copy-start.3
  95.5 28.6 %all-to-all-start.4 = ((f32[8,32,1600]{2,1,0:T(8,128)}), f32[8,32,1600]{2,1,0:T(8,128)S(1)}, u32[]{:S(2)}, u32[]{:S(2)}) async-start(f32[8,32,1600]{2,1,0:T(8,128)} %broadcast_in_dim.24), calls=%async_computation.4 | async-start | bytes 3407872 | tf_op jit(solution)/shard_map/all_to_all | solution.py:35
  127.9 1.2 copy-start.6
  129.1 21.7 %copy-start.7 = (f32[640,640]{1,0:T(8,128)S(1)}, f32[640,640]{1,0:T(8,128)}, u32[]{:S(2)}) copy-start(f32[640,640]{1,0:T(8,128)} %copy-done.6) | copy-start | bytes 4915204
  151.6 0.7 copy-start.8
  175.7 0.7 copy-start.9
  420.4 55.2 %all-to-all-start.9 = ((bf16[8,40,3456]{2,1,0:T(8,128)(2,1)}), bf16[8,40,3456]{2,1,0:T(8,128)(2,1)}, u32[]{:S(2)}, u32[]{:S(2)}) async-start(bf16[8,40,3456]{2,1,0:T(8,128)(2,1)} %broadcast_in_dim.27), calls=%async_computation.9 | async-start | bytes 4423680 | tf_op jit(solution)/shard_map/all_to_all | solution.py:35
  488.3 2.0 copy-start.2
  491.9 11.7 %all-to-all-start.11 = ((f32[4,1,640]{2,1,0:T(1,128)}), f32[4,1,640]{2,1,0:T(1,128)S(1)}, u32[]{:S(2)}, u32[]{:S(2)}) async-start(f32[4,1,640]{2,1,0:T(1,128)} %broadcast_in_dim.31), calls=%async_computation.11 | async-start | bytes 20480 | tf_op jit(solution)/shard_map/all_to_all | solution.py:35
  495.5 4.8 copy-start.4
  498.2 2.1 copy-start.5
  509.1 3.3 copy-start.1
where the time goes:
time: 521 us; the launch traced here: 513 us
  blocking collectives  193 us (37%)
  other arithmetic  167 us (32%)
  waiting for transfers between devices  72.8 us (14%)
  local copies, waits for them, and re-layouts  37.5 us (7%)
  matrix products  23.6 us (5%)
  starting transfers between devices  14.5 us (3%)
    another operation x18, other arithmetic, orthonormal(): chol = jnp.linalg.cholesky(gram)  103 us
    all_to_all x3, waiting for transfers between devices, sent_to_all(): lax.all_to_all(jnp.broadcast_to(x[None], (peers, *x.shape)), axis, 0, 0,...  72.8 us
    all_to_all x1, blocking collectives, sum_in_two_steps_2(): lax.all_to_all(nearer.astype(jnp.bfloat16), far, split_axis=0, concat_axi...  58.4 us
    all_to_all x4, blocking collectives, sent_to_all(): lax.all_to_all(jnp.broadcast_to(x[None], (peers, *x.shape)), axis, 0, 0,...  56.8 us
    another operation x3, other arithmetic, orthonormal(): lax.linalg.triangular_solve(chol, left, left_side=False, lower=True, tran...  50.1 us
    all_to_all x2, blocking collectives, sum_at_owner(): parts = lax.all_to_all(in_blocks(x, dim, peers), axis, 0, 0, tiled=True)  49.2 us
    all_to_all x1, blocking collectives, sum_in_two_steps(): return jnp.sum(lax.all_to_all(own, far, 0, 0, tiled=True), axis=0)  18.2 us
    all_to_all x3, starting transfers between devices, sent_to_all(): lax.all_to_all(jnp.broadcast_to(x[None], (peers, *x.shape)), axis, 0, 0,...  14.5 us
  transfers between devices with their start and end apart: 3, of which 2 were waited for; matrix products, arithmetic and copies ran while one was open for 1% of the time, Pallas kernels for 0%

commit v1 on v0

v1 whole, which is shorter than its diff:
```python
import functools

import jax
import jax.numpy as jnp
from jax import lax
from jax.experimental import pallas as pl
from jax.experimental.pallas import tpu as pltpu
from jax.sharding import Mesh
from jax.sharding import PartitionSpec as P

RANK = 640
ROW = ("row_0", "row_1")
PLANE = ("rep", "col")
BLOCK = 128
SUB = 32

keep_factor = 0.6


def dot(a, b, dims, exact=False):
    return lax.dot_general(
        a,
        b,
        (dims, ((), ())),
        precision=lax.Precision.HIGHEST if exact else None,
        preferred_element_type=jnp.float32,
    )


def eliminated(tile, panel, first):
    groups = SUB // 8
    row = lax.broadcasted_iota(jnp.int32, (8, BLOCK), 0)

    def spread(x, at):
        return jnp.broadcast_to(x[at : at + 1, :], (8, BLOCK))

    column = [[None] * groups for _ in range(SUB)]
    factor = [[None] * groups for _ in range(SUB)]
    kept = [panel[8 * g : 8 * g + 8, :] for g in range(groups)]
    pivots = [None] * groups
    for k in range(SUB):
        own, at = divmod(k, 8)
        for g in range(own, groups):
            lone = tile[8 * g : 8 * g + 8, first + k : first + k + 1]
            column[k][g] = jnp.broadcast_to(lone, (8, BLOCK))
        for j in range(k):
            across = spread(column[j][own], at)
            for g in range(own, groups):
                column[k][g] = column[k][g] - factor[j][g] * across
        pivot = spread(column[k][own], at)
        pivots[own] = pivot if at == 0 else jnp.where(row == at, pivot, pivots[own])
        inverse = 1.0 / pivot
        source = spread(kept[own], at)
        for g in range(own, groups):
            scaled = column[k][g] * inverse
            if g == own:
                scaled = jnp.where(row > at, scaled, 0.0)
            factor[k][g] = scaled
            kept[g] = kept[g] - scaled * source
    out = []
    for g in range(groups):
        y = lax.rsqrt(pivots[g])
        y = y * (1.5 - 0.5 * pivots[g] * y * y)
        out.append(kept[g] * y)
    return jnp.concatenate(out, axis=0)


def factor_kernel(blocks, gram_ref, out_ref, tile_ref):
    out_ref[...] = gram_ref[...]
    lane = lax.broadcasted_iota(jnp.int32, (SUB, BLOCK), 1)
    line = lax.broadcasted_iota(jnp.int32, (SUB, BLOCK), 0)
    below = lax.broadcasted_iota(jnp.int32, (BLOCK, BLOCK), 0)
    right = lax.broadcasted_iota(jnp.int32, (BLOCK, BLOCK), 1)

    @pl.loop(0, blocks)
    def _(k):
        here = pl.ds(pl.multiple_of(k * BLOCK, BLOCK), BLOCK)
        tile_ref[...] = out_ref[here, here]
        for s in range(BLOCK // SUB):
            low, high = s * SUB, (s + 1) * SUB
            tile = tile_ref[low:high, :]
            unit = (lane - low == line).astype(jnp.float32)
            panel = jnp.where((lane >= low) & (lane < high), unit, tile)
            done = eliminated(tile, panel, low)
            tile_ref[low:high, :] = done
            if high < BLOCK:
                gone = right[high:, :] // SUB == s
                rest = jnp.where(gone, 0.0, tile_ref[high:, :])
                tile_ref[high:, :] = rest - dot(done.T[high:, :], done, ((1,), (0,)), True)
        own = jnp.where(right <= below, tile_ref[...], 0.0)
        out_ref[here, :] = dot(own, out_ref[here, :], ((1,), (0,)), True)
        out_ref[here, here] = own

        @pl.loop(k + 1, blocks)
        def _(i):
            there = pl.ds(pl.multiple_of(i * BLOCK, BLOCK), BLOCK)
            panel = out_ref[here, there].T
            out_ref[there, here] = jnp.zeros((BLOCK, BLOCK), jnp.float32)
            out_ref[there, :] = out_ref[there, :] - dot(panel, out_ref[here, :], ((1,), (0,)), True)

    for k in range(blocks):
        here = slice(k * BLOCK, (k + 1) * BLOCK)
        whole = out_ref[here, :]
        lower = lax.broadcasted_iota(jnp.int32, whole.shape, 1) <= (
            lax.broadcasted_iota(jnp.int32, whole.shape, 0) + k * BLOCK
        )
        out_ref[here, :] = jnp.where(lower, whole, 0.0)


def inverse_factor(gram):
    size = gram.shape[0]
    return pl.pallas_call(
        functools.partial(factor_kernel, size // BLOCK),
        out_shape=jax.ShapeDtypeStruct((size, size), jnp.float32),
        in_specs=[pl.BlockSpec(memory_space=pltpu.VMEM)],
        out_specs=pl.BlockSpec(memory_space=pltpu.VMEM),
        scratch_shapes=[pltpu.VMEM((BLOCK, BLOCK), jnp.float32)],
        cost_estimate=pl.CostEstimate(
            flops=20_000_000_000, bytes_accessed=8 * size * size, transcendentals=0
        ),
        name="inverse_factor",
    )(gram)


def summed_at_owner(x, axes):
    return jnp.sum(lax.all_to_all(x, axes, 0, 0, tiled=True), axis=0)


def from_all(x, axes):
    peers = lax.axis_size(axes)
    return lax.all_to_all(jnp.broadcast_to(x[None], (peers, *x.shape)), axes, 0, 0, tiled=True)


def from_other_core(x):
    return lax.ppermute(x, "row_1", [(0, 1), (1, 0)])


def sum_over(x, axis):
    peers = lax.axis_size(axis)
    terms = [x] + [
        lax.ppermute(x, axis, [(i, (i + step) % peers) for i in range(peers)])
        for step in range(1, peers)
    ]
    return sum(terms[1:], terms[0])


def both_cores(mine, theirs, first, axis):
    return jnp.stack([jnp.where(first, mine, theirs), jnp.where(first, theirs, mine)], axis)


def shards(acts, grad_out, momentum, q_basis):
    first = lax.axis_index("row_1") == 0
    grad = dot(acts[0], grad_out[0], ((0,), (0,)))
    boosted = (momentum[0].astype(jnp.float32) + grad).astype(jnp.bfloat16)
    height, width = boosted.shape
    replicas, columns = lax.axis_size("rep"), lax.axis_size("col")
    chips = lax.axis_size("row_0")
    plane = replicas * columns
    lines = RANK // plane
    strip = width // replicas
    short = strip // (2 * chips)

    same = jnp.eye(height, dtype=jnp.bfloat16)
    turned = dot(boosted, same, ((0,), (0,))).reshape(replicas, strip, height)
    total = lax.psum_scatter(turned, "rep", scatter_dimension=0, tiled=False)

    partial_left = dot(q_basis, boosted, ((1,), (1,)))
    mine = summed_at_owner(partial_left.reshape(plane, lines, height), PLANE)
    left = from_all(mine, PLANE).reshape(RANK, height)

    halves = dot(mine, left, ((1,), (1,)), True).reshape(2, lines // 2, RANK)
    kept = jnp.where(first, halves[0], halves[1])
    given = jnp.where(first, halves[1], halves[0])
    half = jnp.sum(from_all(kept + from_other_core(given), "row_0"), axis=0)
    known = from_all(half, PLANE)
    gram = both_cores(known, from_other_core(known), first, 1).reshape(RANK, RANK)

    product = dot(total, left, ((1,), (1,)), True)
    product = product.reshape(2, chips, short, RANK).swapaxes(0, 1)
    share = lax.psum_scatter(
        product.reshape(2 * chips, short, RANK), ROW, scatter_dimension=0, tiled=False
    )

    inverse = inverse_factor(gram)
    ortho = dot(left, inverse, ((0,), (1,)), True).astype(jnp.bfloat16)
    piece = (dot(share, inverse, ((1,), (1,)), True) * (1.0 / replicas)).astype(jnp.bfloat16)
    chips_pieces = from_all(piece, "row_0").reshape(chips * short, RANK)
    known_right = from_all(chips_pieces, "rep")
    right = both_cores(known_right, from_other_core(known_right), first, 1).reshape(width, RANK)

    wide = right.astype(jnp.float32)
    squares = sum_over(jnp.sum(wide * wide, axis=0), "col")
    scale = lax.rsqrt(squares / (width * columns) + 1e-06)
    feedback = dot(ortho, right, ((1,), (1,)))
    momentum_next = (boosted.astype(jnp.float32) - (1.0 - keep_factor) * feedback).astype(
        jnp.bfloat16
    )[None]
    q_full = (wide * scale[None, :]).astype(jnp.bfloat16)
    block = RANK // lax.axis_size(ROW)
    wanted = lax.axis_index(ROW) * block + lax.broadcasted_iota(jnp.int32, (block, RANK), 0)
    chosen = (lax.broadcasted_iota(jnp.int32, (block, RANK), 1) == wanted).astype(jnp.bfloat16)
    q_next = dot(chosen, q_full, ((1,), (1,))).astype(jnp.bfloat16)
    height_all = height * lax.axis_size(ROW)
    update = (
        jnp.sqrt(jnp.float32(height_all) / RANK) * dot(ortho, q_full, ((1,), (1,)))
    ).astype(jnp.bfloat16)
    return (momentum_next, q_next, update)


def solution(mesh):
    split = Mesh(
        mesh.devices.reshape(mesh.shape["rep"], 8, 2, mesh.shape["col"]),
        ("rep", "row_0", "row_1", "col"),
    )
    return jax.shard_map(
        shards,
        mesh=split,
        in_specs=(P("rep", None, ROW), P("rep", None, "col"), P("rep", ROW, "col"), P(None, "col")),
        out_specs=(P("rep", ROW, "col"), P(ROW, "col"), P(ROW, "col")),
        check_vma=False,
    )
```

time: 521 us -> 260 us (0.50); the launches traced: 513 us -> 260 us
  other arithmetic: 167 us -> 5.92 us
  blocking collectives: 193 us -> 100 us
  waiting for transfers between devices: 72.8 us -> 37 us
  Pallas kernels: 0 us -> 25.4 us
  local copies, waits for them, and re-layouts: 37.5 us -> 15.3 us
  matrix products: 23.6 us -> 37.2 us
  starting transfers between devices: 14.5 us -> 24.2 us
  between operations: 4.94 us -> 14.2 us
    another operation x21 -> x4, other arithmetic: 153 us -> 3.57 us  [both_cores(): jnp.stack([jnp.where(first, mine, theirs), jnp.where(first, theirs, mine)...]
    all_to_all x9 -> x4, blocking collectives: 193 us -> 100 us  [the longest x3 76.4 us: from_all(): lax.all_to_all(jnp.broadcast_to(x[None], (peers, *x.shape)), axes, 0, 0,...]
    all_to_all x3 -> x2, waiting for transfers between devices: 72.8 us -> 16.3 us  [from_all(): lax.all_to_all(jnp.broadcast_to(x[None], (peers, *x.shape)), axes, 0, 0,...]
    pallas_call x0 -> x1, Pallas kernels: none -> 25.4 us  [inverse_factor(): pl.pallas_call(functools.partial(factor_kernel, size // BLOCK), out_shape...]
    another operation x26 -> x1, local copies, waits for them, and re-layouts: 18.2 us -> 1.4 us  [both_cores(): jnp.stack([jnp.where(first, mine, theirs), jnp.where(first, theirs, mine)...]
    dot_general x6 -> x9, matrix products: 16.9 us -> 33.3 us  [dot(): lax.dot_general(a, b, (dims, ((), ())), precision=lax.Precision.HIGHEST i...]
    reduce_scatter x0 -> x1, waiting for transfers between devices: none -> 14.4 us  [shards(): total = lax.psum_scatter(turned, 'rep', scatter_dimension=0, tiled=False)]
    ppermute x0 -> x6, starting transfers between devices: none -> 10.6 us  [the longest x3 7.24 us: from_other_core(): return lax.ppermute(x, 'row_1', [(0, 1), (1, 0)])]
  transfers between devices with their start and end apart: 3 -> 10, of which waited for: 2 -> 6; matrix products, arithmetic and copies ran while one was open for 1% -> 14% of each run, Pallas kernels for 0% -> 10%
where the time goes in v1:
time: 260 us
  blocking collectives  100 us (38%)
  matrix products  37.2 us (14%)
  waiting for transfers between devices  37 us (14%)
  Pallas kernels  25.4 us (10%)
  starting transfers between devices  24.2 us (9%)
  local copies, waits for them, and re-layouts  15.3 us (6%)
  between operations  14.2 us (5%)
  other arithmetic  5.92 us (2%)
    all_to_all x3, blocking collectives, from_all(): lax.all_to_all(jnp.broadcast_to(x[None], (peers, *x.shape)), axes, 0, 0,...  76.4 us
    dot_general x9, matrix products, dot(): lax.dot_general(a, b, (dims, ((), ())), precision=lax.Precision.HIGHEST i...  33.3 us
    pallas_call x1, Pallas kernels, inverse_factor(): pl.pallas_call(functools.partial(factor_kernel, size // BLOCK), out_shape...  25.4 us
    all_to_all x1, blocking collectives, summed_at_owner(): return jnp.sum(lax.all_to_all(x, axes, 0, 0, tiled=True), axis=0)  23.9 us
    all_to_all x2, waiting for transfers between devices, from_all(): lax.all_to_all(jnp.broadcast_to(x[None], (peers, *x.shape)), axes, 0, 0,...  16.3 us
    reduce_scatter x1, waiting for transfers between devices, shards(): total = lax.psum_scatter(turned, 'rep', scatter_dimension=0, tiled=False)  14.4 us
    all_to_all x2, starting transfers between devices, from_all(): lax.all_to_all(jnp.broadcast_to(x[None], (peers, *x.shape)), axes, 0, 0,...  13.6 us
    ppermute x3, starting transfers between devices, from_other_core(): return lax.ppermute(x, 'row_1', [(0, 1), (1, 0)])  7.24 us
  transfers between devices with their start and end apart: 10, of which 6 were waited for; matrix products, arithmetic and copies ran while one was open for 14% of the time, Pallas kernels for 10%

profile of v1, /device:TPU:1, one launch (start us, length us, event | category | flops | bytes accessed | tf_op | source)
XLA Modules:
  0.0 259.5 jit_solution(2758295125250341944)
XLA Ops:
  7.2 0.0 reduce-scatter.5.cloned.1.call-start
  7.2 1.4 copy-done
  8.6 2.5 fusion.3
  11.1 3.9 %fusion.9 = f32[3456,320]{1,0:T(8,128)} fusion(bf16[320,3456]{1,0:T(8,128)(2,1)S(1)} %fusion.3), kind=kOutput, calls=%fused_computation.26 | convolution fusion | flops 707891200 | bytes 6635520 | tf_op jit(solution)/shard_map/reshape | solution.py:164
  15.1 5.8 %convolution_bitcast_fusion.1 = f32[640,320]{0,1:T(8,128)} fusion(bf16[320,3456]{1,0:T(8,128)(2,1)} %copy-done.1, bf16[640,3456]{1,0:T(8,128)(2,1)} %param.7), kind=kOutput, calls=%fused_computation.17 | convolution fusion | flops 1415577600 | bytes 7454720 | tf_op jit(solution)/shard_map/dot_general | solution.py:21
  20.9 1.5 copy.39
  22.4 23.9 %all_to_all.30 = f32[16,40,320]{2,1,0:T(8,128)} all-to-all(f32[16,40,320]{2,1,0:T(8,128)S(1)} %bitcast.57), channel_id=1, replica_groups=mesh['rep'=4,'row_0'=8,'row_1'=2,'col'=4] {'rep','col'}, dimensions={0} | all-to-all | bytes 1638400 | tf_op jit(solution)/shard_map/all_to_all | solution.py:126
  46.2 1.3 reduce_sum.27
  47.5 1.0 broadcast_in_dim.14
  48.5 5.2 %all-to-all-start.1 = ((f32[16,40,320]{2,1,0:T(8,128)}), f32[16,40,320]{2,1,0:T(8,128)S(1)}, u32[]{:S(2)}, u32[]{:S(2)}) async-start(f32[16,40,320]{2,1,0:T(8,128)} %broadcast_in_dim.14), calls=%async_computation.1 | async-start | bytes 1966080 | tf_op jit(solution)/shard_map/all_to_all | solution.py:131
  53.7 16.3 %all-to-all-done.1 = f32[16,40,320]{2,1,0:T(8,128)S(1)} async-done(((f32[16,40,320]{2,1,0:T(8,128)}), f32[16,40,320]{2,1,0:T(8,128)S(1)}, u32[]{:S(2)}, u32[]{:S(2)}) %all-to-all-start.1) | async-done | bytes 819232 | tf_op jit(solution)/shard_map/all_to_all | solution.py:131
  70.0 1.1 fusion.13
  71.1 3.1 %collective-permute-start = (f32[20,640]{1,0:T(8,128)S(1)}, f32[20,640]{1,0:T(8,128)S(1)}, u32[]{:S(2)}, u32[]{:S(2)}) collective-permute-start(f32[20,640]{1,0:T(8,128)S(1)} %slice_select_fusion), channel_id=1, source_target_pairs={{0,4},{4,0},{1,5},{5,1},{2,6},{6,2},{3,7},{7,3},{8,12},{12,8},{9,1... | collective-permute-start | bytes 153608 | tf_op jit(solution)/shard_map/ppermute | solution.py:135
  74.2 0.9 collective-permute-done
  75.1 0.8 broadcast_in_dim.15
  76.0 8.4 %all-to-all-start.2 = ((f32[8,20,640]{2,1,0:T(8,128)}), f32[8,20,640]{2,1,0:T(8,128)S(1)}, u32[]{:S(2)}, u32[]{:S(2)}) async-start(f32[8,20,640]{2,1,0:T(8,128)} %broadcast_in_dim.15), calls=%async_computation.2 | async-start | bytes 983040 | tf_op jit(solution)/shard_map/all_to_all | solution.py:131
  84.4 14.4 %reduce-scatter.5.cloned.1.call-done = f32[1,864,320]{2,1,0:T(8,128)} async-done(((f32[4,864,320]{2,1,0:T(8,128)}), f32[1,864,320]{2,1,0:T(8,128)}) %reduce-scatter.5.cloned.1.call-update) | async-done | bytes 1105936 | tf_op jit(solution)/shard_map/reduce_scatter | solution.py:165
  98.8 2.6 dot_general.40
  101.3 5.7 %convolution_bitcast_fusion = f32[8,2,54,640]{3,2,0,1:T(8,128)S(1)} fusion(f32[2,8,54,320]{3,2,1,0:T(8,128)} %dot_general.40, f32[640,320,1,1]{1,0,3,2:T(8,128)S(1)} %bitcast.51), kind=kOutput, calls=%fused_computation.16 | convolution fusion | flops 2123366400 | bytes 4136960 | tf_op jit(solution)/shard_map/dot_general | solution.py:21
  107.0 1.5 copy.47
  108.6 0.1 broadcast_in_dim.16
  108.7 20.3 %all_to_all.31 = f32[16,20,640]{2,1,0:T(8,128)S(1)} all-to-all(f32[16,20,640]{2,1,0:T(8,128)S(1)} %broadcast_in_dim.16), channel_id=1, replica_groups=mesh['rep'=4,'row_0'=8,'row_1'=2,'col'=4] {'rep','col'}, dimensions={0} | all-to-all | bytes 1638400 | tf_op jit(solution)/shard_map/all_to_all | solution.py:131
  129.0 0.2 copy.41
  129.2 2.1 collective-permute-start.1
  131.3 2.1 collective-permute-done.1
  133.4 0.3 fusion.7
  133.6 0.1 pad_maximum_fusion.1
  133.8 1.4 copy.44
  135.2 2.6 reshape.42.gram_ref
  137.8 25.4 %inverse_factor.1 = f32[640,640]{1,0:T(8,128)} custom-call(f32[640,640]{1,0:T(8,128)} %reshape.42.gram_ref), custom_call_target="tpu_custom_call" | custom-call | flops 20000000000 | bytes 3276800 | tf_op jit(solution)/shard_map/inverse_factor/pallas_call | solution.py:112
  163.2 3.1 %reduce-scatter.7.cloned.1.call-done = f32[1,54,640]{2,1,0:T(8,128)} async-done(((f32[16,54,640]{2,1,0:T(8,128)}), f32[1,54,640]{2,1,0:T(8,128)}) %reduce-scatter.7.cloned.1.call-update) | async-done | bytes 138256
  166.3 3.2 %fusion.6 = bf16[54,640]{1,0:T(8,128)(2,1)S(1)} fusion(f32[640,640]{1,0:T(8,128)} %inverse_factor.1, f32[1,54,640]{2,1,0:T(8,128)} %reduce-scatter.7.cloned.1.call-done), kind=kOutput, calls=%fused_computation.20 | convolution fusion | flops 265489920 | bytes 1845760 | tf_op jit(solution)/shard_map/dot_general | solution.py:21
  169.6 26.3 %all_to_all.32 = bf16[8,54,640]{2,1,0:T(8,128)(2,1)S(1)} all-to-all(bf16[8,54,640]{2,1,0:T(8,128)(2,1)S(1)} %broadcast_in_dim.17), channel_id=1, replica_groups=mesh['rep'=4,'row_0'=8,'row_1'=2,'col'=4] {'row_0'}, dimensions={0} | all-to-all | bytes 1105920 | tf_op jit(solution)/shard_map/all_to_all | solution.py:131
  195.9 0.9 broadcast_in_dim.18
  196.8 1.2 broadcast_in_dim.19
  198.1 29.7 %all_to_all.33 = bf16[4,432,640]{2,1,0:T(8,128)(2,1)} all-to-all(bf16[4,432,640]{2,1,0:T(8,128)(2,1)S(1)} %broadcast_in_dim.19), channel_id=1, replica_groups=mesh['rep'=4,'row_0'=8,'row_1'=2,'col'=4] {'rep'}, dimensions={0} | all-to-all | bytes 4423680 | tf_op jit(solution)/shard_map/all_to_all | solution.py:131
  227.8 2.0 collective-permute-start.2
  229.8 6.2 %convolution_convert_fusion.1 = bf16[320,640]{1,0:T(8,128)(2,1)S(1)} fusion(f32[640,320]{1,0:T(8,128)S(1)} %bitcast.52, f32[640,640]{1,0:T(8,128)} %inverse_factor.1), kind=kOutput, calls=%fused_computation.18 | convolution fusion | flops 1573068800 | bytes 2867200 | tf_op jit(solution)/shard_map/dot_general | solution.py:21
  236.1 2.7 %select_bitcast_fusion.1 = (bf16[4,1,432,640]{3,2,1,0:T(8,128)(2,1)S(1)}, bf16[4,1,432,640]{3,2,1,0:T(8,128)(2,1)S(1)}) fusion(bf16[4,432,640]{2,1,0:T(8,128)(2,1)} %all_to_all.33, bf16[4,432,640]{2,1,0:T(8,128)(2,1)} %collective-permute-done.2, pred[]{:T(512)S(6)} %eq.9), kind=kLoop, calls=%fused_computation.13 | loop fusion | flops 2211840 | bytes 8847361 | tf_op jit(solution)/shard_map/stack | solution.py:148
  238.8 1.0 multiply_reduce_fusion
  239.8 0.5 pad_maximum_fusion
  240.2 2.2 collective-permute-start.5
  242.5 0.7 collective-permute-start.4
  243.2 0.4 collective-permute-start.3
  243.6 3.3 %fusion.4 = bf16[1,320,3456]{2,1,0:T(8,128)(2,1)} fusion(bf16[320,640]{1,0:T(8,128)(2,1)S(1)} %convolution_convert_fusion.1, bf16[3456,640]{1,0:T(8,128)(2,1)S(1)} %bitcast.54, bf16[320,3456]{1,0:T(8,128)(2,1)S(1)} %copy-done.2), kind=kOutput, calls=%fused_computation.9 | convolution fusion | flops 1420001280 | bytes 9256960 | tf_op jit(solution)/shard_map/dot_general | solution.py:21
  246.9 0.2 collective-permute-done.3
  247.2 3.3 %fusion.2 = bf16[320,3456]{1,0:T(8,128)(2,1)} fusion(bf16[320,640]{1,0:T(8,128)(2,1)S(1)} %convolution_convert_fusion.1, bf16[3456,640]{1,0:T(8,128)(2,1)S(1)} %bitcast.55, f32[640]{0:T(1024)S(1)} %add_rsqrt_fusion), kind=kOutput, calls=%fused_computation.7 | convolution fusion | flops 1424424960 | bytes 7047680 | tf_op jit(solution)/shard_map/dot_general | solution.py:21
  250.5 2.2 convolution_convert_fusion
  (18 shorter events, 0.2 us)
Async XLA Ops:
  7.2 1.5 copy-start
  7.2 91.6 %reduce-scatter.5.cloned.1.call-start = ((), (), s32[]{:S(2)}) async-start(), calls=%async_computation.8 | async-start | bytes 6635520 | tf_op jit(solution)/shard_map/reduce_scatter | solution.py:165
  11.1 3.9 %copy-start.1 = (bf16[320,3456]{1,0:T(8,128)(2,1)}, bf16[320,3456]{1,0:T(8,128)(2,1)S(1)}, u32[]{:S(2)}) copy-start(bf16[320,3456]{1,0:T(8,128)(2,1)S(1)} %fusion.3) | copy-start | bytes 6635524
  48.5 21.5 %all-to-all-start.1 = ((f32[16,40,320]{2,1,0:T(8,128)}), f32[16,40,320]{2,1,0:T(8,128)S(1)}, u32[]{:S(2)}, u32[]{:S(2)}) async-start(f32[16,40,320]{2,1,0:T(8,128)} %broadcast_in_dim.14), calls=%async_computation.1 | async-start | bytes 1966080 | tf_op jit(solution)/shard_map/all_to_all | solution.py:131
  71.1 4.0 %collective-permute-start = (f32[20,640]{1,0:T(8,128)S(1)}, f32[20,640]{1,0:T(8,128)S(1)}, u32[]{:S(2)}, u32[]{:S(2)}) collective-permute-start(f32[20,640]{1,0:T(8,128)S(1)} %slice_select_fusion), channel_id=1, source_target_pairs={{0,4},{4,0},{1,5},{5,1},{2,6},{6,2},{3,7},{7,3},{8,12},{12,8},{9,1... | collective-permute-start | bytes 153608 | tf_op jit(solution)/shard_map/ppermute | solution.py:135
  76.0 32.6 %all-to-all-start.2 = ((f32[8,20,640]{2,1,0:T(8,128)}), f32[8,20,640]{2,1,0:T(8,128)S(1)}, u32[]{:S(2)}, u32[]{:S(2)}) async-start(f32[8,20,640]{2,1,0:T(8,128)} %broadcast_in_dim.15), calls=%async_computation.2 | async-start | bytes 983040 | tf_op jit(solution)/shard_map/all_to_all | solution.py:131
  84.3 82.0 %reduce-scatter.7.cloned.1.call-start = ((), (), s32[]{:S(2)}) async-start(), calls=%async_computation.9 | async-start | bytes 2437120
  129.2 4.2 %collective-permute-start.1 = (f32[16,20,640]{2,0,1:T(8,128)S(1)}, f32[16,20,640]{2,0,1:T(8,128)S(1)}, u32[]{:S(2)}, u32[]{:S(2)}) collective-permute-start(f32[16,20,640]{2,0,1:T(8,128)S(1)} %copy.41), channel_id=1, source_target_pairs={{0,4},{4,0},{1,5},{5,1},{2,6},{6,2},{3,7},{7,3},{8,12},{12,8},{9,1... | collective-permute-start | bytes 2457608 | tf_op jit(solution)/shard_map/ppermute | solution.py:135
  227.8 8.2 %collective-permute-start.2 = (bf16[4,432,640]{2,1,0:T(8,128)(2,1)}, bf16[4,432,640]{2,1,0:T(8,128)(2,1)}, u32[]{:S(2)}, u32[]{:S(2)}) collective-permute-start(bf16[4,432,640]{2,1,0:T(8,128)(2,1)} %all_to_all.33), channel_id=1, source_target_pairs={{0,4},{4,0},{1,5},{5,1},{2,6},{6,2},{3,7},{7,3},{8,12},{12,8},{9,1... | collective-permute-start | bytes 6635528 | tf_op jit(solution)/shard_map/ppermute | solution.py:135
  239.8 3.8 %copy-start.2 = (bf16[320,3456]{1,0:T(8,128)(2,1)S(1)}, bf16[320,3456]{1,0:T(8,128)(2,1)}, u32[]{:S(2)}) copy-start(bf16[320,3456]{1,0:T(8,128)(2,1)} %copy-done.1) | copy-start | bytes 6635524
  240.2 6.7 %collective-permute-start.5 = (f32[640]{0:T(1024)S(1)}, f32[640]{0:T(1024)S(1)}, u32[]{:S(2)}, u32[]{:S(2)}) collective-permute-start(f32[640]{0:T(1024)S(1)} %multiply_reduce_fusion), channel_id=1, source_target_pairs={{0,3},{1,0},{2,1},{3,2},{4,7},{5,4},{6,5},{7,6},{8,11},{9,8},{10,9... | collective-permute-start | bytes 7688 | tf_op jit(solution)/shard_map/ppermute | solution.py:141
  242.5 4.4 %collective-permute-start.4 = (f32[640]{0:T(1024)S(1)}, f32[640]{0:T(1024)S(1)}, u32[]{:S(2)}, u32[]{:S(2)}) collective-permute-start(f32[640]{0:T(1024)S(1)} %multiply_reduce_fusion), channel_id=1, source_target_pairs={{0,2},{1,3},{2,0},{3,1},{4,6},{5,7},{6,4},{7,5},{8,10},{9,11},{10,... | collective-permute-start | bytes 7688 | tf_op jit(solution)/shard_map/ppermute | solution.py:141
  243.2 4.0 %collective-permute-start.3 = (f32[640]{0:T(1024)S(1)}, f32[640]{0:T(1024)S(1)}, u32[]{:S(2)}, u32[]{:S(2)}) collective-permute-start(f32[640]{0:T(1024)S(1)} %multiply_reduce_fusion), channel_id=1, source_target_pairs={{0,1},{1,2},{2,3},{3,0},{4,5},{5,6},{6,7},{7,4},{8,9},{9,10},{10,1... | collective-permute-start | bytes 7688 | tf_op jit(solution)/shard_map/ppermute | solution.py:141
Sparse Core Ops, SparseCore 0:
  15.2 83.5 reduce-scatter.4
  108.7 57.5 reduce-scatter.6
